TPU v7x, 32 devices: a whole 2x2x4 slice. The times are simulated.
32 devices in a mesh: dp: 2 (over x), fsdp: 4 (over z), ep: 4 (over y, core).
Axes of the slice: x: 2, y: 2, z: 4, core: 2. Of those that a mesh axis runs over, the one named last changes fastest.
Arguments:
- hidden: bfloat16 [65536, 4096], P(('dp', 'fsdp', 'ep')), parts along dimension 0
- norm_gain: bfloat16 [4096], replicated
- w_router: bfloat16 [4096, 8], replicated
- w_gate: bfloat16 [8, 4096, 1376], P('ep', 'fsdp')
- w_up: bfloat16 [8, 4096, 1376], P('ep', 'fsdp')
- w_down: bfloat16 [8, 1376, 4096], P('ep', None, 'fsdp')
- top2_ids: int32 [65536, 2], P(('dp', 'fsdp', 'ep')), parts along dimension 0
Outputs:
- output: bfloat16 [65536, 4096], P(('dp', 'fsdp', 'ep')), parts along dimension 0
There are 2 independent parts. A program takes and returns all parts, laid end to end along the dimension named above; an argument that names none is the same for every part.
All inputs are finite; a program needn't handle non-finite values.
Results may differ from a plain program's by a relative error of at most 0.001.
Values are sent between devices in bfloat16 or wider.
A program may use at most 1 GiB of HBM per device.

v0:
```python
import jax
import jax.numpy as jnp
from jax import lax
from jax.sharding import PartitionSpec as P

EPS = 1e-5


def norm_and_gates(hidden, norm_gain, w_router, top2_ids):
    hidden_f32 = hidden.astype(jnp.float32)
    mean_sq = jnp.mean(hidden_f32 * hidden_f32, axis=-1, keepdims=True)
    normed = (hidden_f32 * lax.rsqrt(mean_sq + EPS) * norm_gain.astype(jnp.float32)).astype(jnp.bfloat16)
    logits = jnp.dot(normed, w_router, preferred_element_type=jnp.float32)
    gate_probs = jax.nn.softmax(jnp.take_along_axis(logits, top2_ids, axis=1), axis=-1)
    return hidden_f32, normed, gate_probs


def route_slots(top2_ids, num_experts, capacity):
    flat_ids = top2_ids.reshape(-1)
    onehot = (flat_ids[:, None] == jnp.arange(num_experts, dtype=jnp.int32)[None, :]).astype(jnp.int32)
    position = jnp.sum((jnp.cumsum(onehot, axis=0) - 1) * onehot, axis=1)
    slot_ids = jnp.where(position < capacity, flat_ids * capacity + position, num_experts * capacity)
    return slot_ids.reshape(top2_ids.shape)


def gather_rows(normed, slot_ids, num_slots):
    tok_count = slot_ids.shape[0]
    token_index = jnp.broadcast_to(jnp.arange(tok_count, dtype=jnp.int32)[:, None], slot_ids.shape)
    source = jnp.full((num_slots,), tok_count, dtype=jnp.int32).at[slot_ids.reshape(-1)].set(token_index.reshape(-1), mode='drop')
    return jnp.take(normed, source, axis=0, mode='fill', fill_value=0)


def take_slots(expert_rows, slot_ids):
    return jnp.take(expert_rows, slot_ids, axis=0, mode='fill', fill_value=0)


def expert_block(rows_in, gate_full, up_full, down_full):
    act_a = jnp.einsum('ecd,edf->ecf', rows_in, gate_full, preferred_element_type=jnp.float32)
    act_b = jnp.einsum('ecd,edf->ecf', rows_in, up_full, preferred_element_type=jnp.float32)
    hidden_act = (jax.nn.silu(act_a) * act_b).astype(jnp.bfloat16)
    return jnp.einsum('ecf,efd->ecd', hidden_act, down_full, preferred_element_type=jnp.float32).astype(jnp.bfloat16)


def local_block(hidden, norm_gain, w_router, w_gate, w_up, w_down, top2_ids):
    tok_local, d_model = hidden.shape
    num_experts = w_router.shape[1]
    capacity = (5 * tok_local + 2 * num_experts - 1) // (2 * num_experts)
    hidden_f32, normed, gate_probs = norm_and_gates(hidden, norm_gain, w_router, top2_ids)
    slot_ids = route_slots(top2_ids, num_experts, capacity)
    send_rows = gather_rows(normed, slot_ids, num_experts * capacity).reshape(num_experts, capacity, d_model)
    gate_full = lax.all_gather(w_gate, 'fsdp', axis=1, tiled=True)
    up_full = lax.all_gather(w_up, 'fsdp', axis=1, tiled=True)
    down_full = lax.all_gather(w_down, 'fsdp', axis=2, tiled=True)
    recv_rows = lax.all_to_all(send_rows, 'ep', 0, 1, tiled=True)
    expert_out = expert_block(recv_rows, gate_full, up_full, down_full)
    back_rows = lax.all_to_all(expert_out, 'ep', 1, 0, tiled=True)
    returned = take_slots(back_rows.reshape(num_experts * capacity, d_model), slot_ids)
    moe_sum = jnp.sum(gate_probs[:, :, None] * returned.astype(jnp.float32), axis=1)
    return (hidden_f32 + moe_sum).astype(jnp.bfloat16)


def solution(mesh):
    tok_spec = P(('dp', 'fsdp', 'ep'), None)
    in_specs = (tok_spec, P(None), P(None, None), P('ep', 'fsdp', None), P('ep', 'fsdp', None), P('ep', None, 'fsdp'), tok_spec)
    return jax.shard_map(local_block, mesh=mesh, in_specs=in_specs, out_specs=tok_spec, check_vma=False)
```

profile of v0, /device:TPU:2, one launch (start us, length us, event | category | flops | bytes accessed | tf_op | source)
XLA Modules:
  0.0 2167.1 jit_solution(11848179975228375337)
XLA Ops:
  6.5 0.0 copy-start
  6.5 0.0 all-gather.4.cloned.1.call-start
  6.5 0.7 all-gather.4.cloned.1.call-update
  7.3 0.0 all-gather.6.cloned.1.call-start
  7.3 0.7 all-gather.6.cloned.1.call-update
  8.0 1.1 copy.35
  9.1 0.5 eq.29
  9.6 0.5 eq.25
  10.0 2.3 reduce-window.6
  12.4 0.3 slice_reduce_fusion
  12.7 0.2 reduce-window.9
  12.9 0.7 broadcast_multiply_fusion
  13.6 0.4 copy.40
  14.0 0.6 mul.59
  14.6 0.1 broadcast_in_dim.57
  14.7 0.5 reshape.148
  15.1 0.7 convert_element_type.27
  15.8 0.1 add_bitcast_fusion
  15.9 0.1 fusion.5
  16.1 0.0 copy-start.4
  16.1 0.5 copy-done.4
  16.7 15.5 scatter_custom_fusion
  32.3 0.0 copy-start.1
  32.3 7.5 fusion
  39.8 3.1 copy-done.1
  42.9 8.6 fusion.2
  51.6 77.3 %gather_fusion = bf16[5120,4096]{1,0:T(8,128)(2,1)} fusion(bf16[2048,4096]{1,0:T(8,128)(2,1)} %fusion.2, s32[5120]{0:T(1024)S(1)} %fusion.7), kind=kCustom, calls=%fused_computation | custom fusion | bytes 83906560 | tf_op jit(solution)/shard_map/jit(_take)/gather | solution.py:30
  128.9 28.2 %broadcast_select_fusion.1 = bf16[8,640,4096]{2,1,0:T(8,128)(2,1)} fusion(bf16[8,640,4096]{2,1,0:T(8,128)(2,1)} %bitcast.39, pred[8,640]{1,0:T(8,128)(4,1)S(1)} %broadcast_in_dim.58), kind=kLoop, calls=%fused_computation.9 | loop fusion | flops 20971520 | bytes 83891200 | tf_op jit(solution)/shard_map/jit(_take)/select_n | solution.py:30
  157.1 11.2 all-to-all-start
  168.2 0.5 all-gather.8.cloned.1.call-start
  168.8 0.2 all-gather.8.cloned.1.call-update
  169.0 451.6 %all-to-all-done = bf16[8,640,4096]{2,1,0:T(8,128)(2,1)} async-done(((bf16[8,640,4096]{2,1,0:T(8,128)(2,1)}), bf16[8,640,4096]{2,1,0:T(8,128)(2,1)}, u32[]{:S(2)}, u32[]{:S(2)}) %all-to-all-start) | async-done | bytes 41943072 | tf_op jit(solution)/shard_map/all_to_all | solution.py:54
  620.6 28.2 %copy.41 = bf16[2,4,640,4096]{3,2,1,0:T(8,128)(2,1)} copy(bf16[2,4,640,4096]{3,2,0,1:T(8,128)(2,1)} %bitcast.6) | data formatting | bytes 83886080 | tf_op jit(solution)/shard_map/all_to_all | solution.py:54
  648.8 68.1 %fusion.14 = f32[2,2560,1376]{1,2,0:T(8,128)} fusion(bf16[2,2560,4096]{2,1,0:T(8,128)(2,1)} %bitcast.40, bf16[2,4096,1376]{1,2,0:T(8,128)(2,1)} %all-gather.4.cloned.1.call-done), kind=kOutput, calls=%fused_computation.45 | convolution fusion | flops 57713623040 | bytes 92667904 | tf_op jit(solution)/shard_map/ecd,edf->ecf/dot_general | solution.py:38
  716.8 60.1 %all-gather.6.cloned.1.call-done = bf16[2,4096,1376]{1,2,0:T(8,128)(2,1)} async-done(((bf16[2,1024,1376]{1,2,0:T(8,128)(2,1)}), bf16[2,4096,1376]{1,2,0:T(8,128)(2,1)}) %all-gather.6.cloned.1.call-update) | async-done | bytes 22544400 | tf_op jit(solution)/shard_map/all_gather | solution.py:52
  776.9 76.3 %multiply_convert_fusion = bf16[2,2560,1376]{1,2,0:T(8,128)(2,1)} fusion(f32[2,2560,1376]{1,2,0:T(8,128)} %fusion.14, bf16[2,2560,4096]{2,1,0:T(8,128)(2,1)} %bitcast.41, bf16[2,4096,1376]{1,2,0:T(8,128)(2,1)} %all-gather.6.cloned.1.call-done), kind=kOutput, calls=%fused_computation.15 | convolution fusion | flops 57755893760 | bytes 106758144 | tf_op jit(solution)/shard_map/ecd,edf->ecf/dot_general | solution.py:39
  853.2 307.2 %all-gather.8.cloned.1.call-done = bf16[2,1376,4096]{2,1,0:T(8,128)(2,1)} async-done(((bf16[2,1376,1024]{2,1,0:T(8,128)(2,1)}), bf16[2,1376,4096]{2,1,0:T(8,128)(2,1)}) %all-gather.8.cloned.1.call-update) | async-done | bytes 22544400 | tf_op jit(solution)/shard_map/all_gather | solution.py:53
  1160.4 73.5 %convolution_convert_fusion = bf16[2,2560,4096]{2,1,0:T(8,128)(2,1)} fusion(bf16[2,2560,1376]{1,2,0:T(8,128)(2,1)} %multiply_convert_fusion, bf16[2,1376,4096]{2,1,0:T(8,128)(2,1)} %all-gather.8.cloned.1.call-done), kind=kOutput, calls=%fused_computation.14 | convolution fusion | flops 57734594560 | bytes 78577664 | tf_op jit(solution)/shard_map/ecf,efd->ecd/dot_general | solution.py:41
  1233.9 74.7 %copy.42 = bf16[2,2560,4096]{2,0,1:T(2,128)(2,1)} copy(bf16[2,2560,4096]{2,1,0:T(8,128)(2,1)} %convolution_convert_fusion) | data formatting | bytes 83886080 | tf_op jit(solution)/shard_map/convert_element_type | solution.py:41
  1308.6 11.6 all-to-all-start.1
  1320.1 0.0 copy-done.5
  1320.2 1.0 reduce_sum.43
  1321.2 0.3 copy.37
  1321.5 0.0 copy-done.2
  1321.5 0.6 compare_and_fusion
  1322.1 0.4 copy.44
  1322.5 1.1 reshape.132
  1323.6 0.4 copy.32
  1324.0 0.5 reshape.138
  1324.5 0.0 copy-done
  1324.5 10.2 fusion.13
  1334.7 24.5 %gather_fusion.2 = f32[4096]{0:T(1024)S(1)} fusion(f32[2048,8]{0,1:T(8,128)S(1)} %fusion.13, s32[4096]{0:T(1024)S(1)} %reshape.138), kind=kCustom, calls=%fused_computation.2 | custom fusion | bytes 65536 | tf_op jit(solution)/shard_map/jit(take_along_axis)/gather | solution.py:14
  1359.2 1.0 reshape.141
  1360.2 0.3 copy.33
  1360.5 0.0 copy-done.3
  1360.7 0.4 copy.34
  1361.0 0.0 copy-done.7
  1361.1 0.5 copy.39
  1361.6 410.9 %all-to-all-done.1 = bf16[2,2560,4096]{2,0,1:T(2,128)(2,1)} async-done(((bf16[2,2560,4096]{2,0,1:T(2,128)(2,1)}), bf16[2,2560,4096]{2,0,1:T(2,128)(2,1)}, u32[]{:S(2)}, u32[]{:S(2)}) %all-to-all-start.1) | async-done | bytes 41943072 | tf_op jit(solution)/shard_map/all_to_all | solution.py:56
  1772.5 36.4 %copy.43 = bf16[2,4,640,4096]{3,2,0,1:T(8,128)(2,1)} copy(bf16[2,4,640,4096]{3,0,2,1:T(2,128)(2,1)} %bitcast.8) | data formatting | bytes 83886080 | tf_op jit(solution)/shard_map/all_to_all | solution.py:56
  1808.9 149.5 %gather_fusion.1 = bf16[4096,4096]{1,0:T(8,128)(2,1)} fusion(bf16[5120,4096]{1,0:T(8,128)(2,1)} %bitcast.38, s32[4096]{0:T(1024)S(1)} %broadcast_clamp_fusion), kind=kCustom, calls=%fused_computation.1 | custom fusion | bytes 67125248 | tf_op jit(solution)/shard_map/jit(_take)/gather | solution.py:34
  1958.4 53.1 %reshape.131 = bf16[2048,2,4096]{2,1,0:T(2,128)(2,1)} reshape(bf16[4096,4096]{1,0:T(8,128)(2,1)} %gather_fusion.1) | data formatting | bytes 67108864 | tf_op jit(solution)/shard_map/jit(_take)/gather | solution.py:34
  2011.5 126.7 %multiply_reduce_fusion = f32[2048,4096]{1,0:T(8,128)} fusion(bf16[2048,2,4096]{2,1,0:T(2,128)(2,1)} %reshape.131, pred[2048,2]{1,0:T(8,128)(4,1)S(1)} %copy.39, f32[2048,2]{1,0:T(8,128)S(1)} %copy.34), kind=kLoop, calls=%fused_computation.4 | loop fusion | flops 58720256 | bytes 67129344 | tf_op jit(solution)/shard_map/reduce_sum | solution.py:58
  2138.1 22.0 %fusion.3 = bf16[2048,4096]{1,0:T(8,128)(2,1)} fusion(f32[2048,4096]{1,0:T(8,128)} %multiply_reduce_fusion, bf16[2048,4096]{1,0:T(8,128)(2,1)} %param.7), kind=kLoop, calls=%fused_computation.13 | loop fusion | flops 25165824 | bytes 67108864 | tf_op jit(solution)/shard_map/convert_element_type | solution.py:59
  (18 shorter events, 0.3 us)
Async XLA Ops:
  6.5 1317.9 %copy-start = (bf16[4096,8]{0,1:T(8,128)(2,1)S(1)}, bf16[4096,8]{0,1:T(8,128)(2,1)}, u32[]{:S(2)}) copy-start(bf16[4096,8]{0,1:T(8,128)(2,1)} %param.9) | copy-start | bytes 196612
  6.5 642.2 %all-gather.4.cloned.1.call-start = ((), (), s32[]{:S(2)}) async-start(), calls=%async_computation.2 | async-start | bytes 28180480 | tf_op jit(solution)/shard_map/all_gather | solution.py:51
  7.3 769.7 %all-gather.6.cloned.1.call-start = ((), (), s32[]{:S(2)}) async-start(), calls=%async_computation.3 | async-start | bytes 28180480 | tf_op jit(solution)/shard_map/all_gather | solution.py:52
  16.1 0.6 copy-start.4
  32.3 10.7 copy-start.1
  157.1 463.5 %all-to-all-start = ((bf16[8,640,4096]{2,1,0:T(8,128)(2,1)}), bf16[8,640,4096]{2,1,0:T(8,128)(2,1)}, u32[]{:S(2)}, u32[]{:S(2)}) async-start(bf16[8,640,4096]{2,1,0:T(8,128)(2,1)} %broadcast_select_fusion.1), calls=%async_computation | async-start | bytes 83886080 | tf_op jit(solution)/shard_map/all_to_all | solution.py:54
  168.2 992.2 %all-gather.8.cloned.1.call-start = ((), (), s32[]{:S(2)}) async-start(), calls=%async_computation.4 | async-start | bytes 28180480 | tf_op jit(solution)/shard_map/all_gather | solution.py:53
  1308.6 11.6 copy-start.5
  1308.6 12.9 copy-start.2
  1308.6 463.9 %all-to-all-start.1 = ((bf16[2,2560,4096]{2,0,1:T(2,128)(2,1)}), bf16[2,2560,4096]{2,0,1:T(2,128)(2,1)}, u32[]{:S(2)}, u32[]{:S(2)}) async-start(bf16[2,2560,4096]{2,0,1:T(2,128)(2,1)} %copy.42), calls=%async_computation.1 | async-start | bytes 83886080 | tf_op jit(solution)/shard_map/all_to_all | solution.py:56
  1334.7 25.9 %copy-start.3 = (s32[2048,2]{0,1:T(2,128)S(1)}, s32[2048,2]{0,1:T(2,128)}, u32[]{:S(2)}) copy-start(s32[2048,2]{0,1:T(2,128)} %param.13) | copy-start | bytes 49156
  1334.7 26.4 %copy-start.7 = (pred[2048,2]{0,1:T(4,128)(4,1)S(1)}, pred[2048,2]{0,1:T(4,128)(4,1)}, u32[]{:S(2)}) copy-start(pred[2048,2]{0,1:T(4,128)(4,1)} %get-tuple-element.7) | copy-start | bytes 12292
  1334.7 26.9 %copy-start.6 = (s32[4096]{0:T(1024)S(1)}, s32[4096]{0:T(1024)}, u32[]{:S(2)}) copy-start(s32[4096]{0:T(1024)} %reshape.132) | copy-start | bytes 49156
Sparse Core Ops, SparseCore 0:
  8.9 384.5 all-gather.3
  395.1 381.8 all-gather.5
  778.5 381.8 all-gather.7
where the time goes:
time: 2180 us; the launch traced here: 2170 us
  waiting for transfers between devices  1230 us (56%)
  local copies, waits for them, and re-layouts  473 us (22%)
  matrix products  228 us (10%)
  other arithmetic  198 us (9%)
  starting transfers between devices  23.3 us (1%)
    all_to_all x1, waiting for transfers between devices, local_block(): recv_rows = lax.all_to_all(send_rows, 'ep', 0, 1, tiled=True)  452 us
    all_to_all x1, waiting for transfers between devices, local_block(): back_rows = lax.all_to_all(expert_out, 'ep', 1, 0, tiled=True)  411 us
    all_gather x1, waiting for transfers between devices, local_block(): down_full = lax.all_gather(w_down, 'fsdp', axis=2, tiled=True)  307 us
    gather x2, local copies, waits for them, and re-layouts, take_slots(): return jnp.take(expert_rows, slot_ids, axis=0, mode='fill', fill_value=0)  203 us
    reduce_sum x1, other arithmetic, local_block(): jnp.sum(gate_probs[:, :, None] * returned.astype(jnp.float32), axis=1)  127 us
    gather x1, local copies, waits for them, and re-layouts, gather_rows(): return jnp.take(normed, source, axis=0, mode='fill', fill_value=0)  77.3 us
    dot_general x1, matrix products, expert_block(): jnp.einsum('ecd,edf->ecf', rows_in, up_full, preferred_element_type=jnp.f...  76.3 us
    convert_element_type x1, local copies, waits for them, and re-layouts, expert_block(): jnp.einsum('ecf,efd->ecd', hidden_act, down_full, preferred_element_type=...  74.7 us
  transfers between devices with their start and end apart: 5, of which 4 were waited for; matrix products, arithmetic and copies ran while one was open for 17% of the time, Pallas kernels for 0%

commit v1 on v0

v1 whole, which is shorter than its diff:
```python
import functools

import jax
import jax.numpy as jnp
from jax import lax
from jax.experimental import pallas as pl
from jax.experimental.pallas import tpu as pltpu
from jax.sharding import PartitionSpec as P

EPS = 1e-5
CHUNK = 256
WINDOW = 128
SPAN = 160
BUFFERS = 4
VMEM_LIMIT = 63 * 1024 * 1024
NT = (((1,), (1,)), ((), ()))


def norm_rows(hidden, norm_gain):
    hidden_f32 = hidden.astype(jnp.float32)
    mean_sq = jnp.mean(hidden_f32 * hidden_f32, axis=-1, keepdims=True)
    return (hidden_f32 * lax.rsqrt(mean_sq + EPS) * norm_gain.astype(jnp.float32)).astype(jnp.bfloat16)


def expert_gates(normed, w_router, top2_ids, order):
    logits = jnp.dot(normed, w_router, preferred_element_type=jnp.float32)
    experts = jnp.arange(w_router.shape[1], dtype=jnp.int32)[None, :]
    hit_0 = top2_ids[:, 0:1] == experts
    hit_1 = top2_ids[:, 1:2] == experts
    r_0 = jnp.sum(jnp.where(hit_0, logits, 0.0), axis=1, keepdims=True)
    r_1 = jnp.sum(jnp.where(hit_1, logits, 0.0), axis=1, keepdims=True)
    top = jnp.maximum(r_0, r_1)
    x_0, x_1 = jnp.exp(r_0 - top), jnp.exp(r_1 - top)
    total = x_0 + x_1
    at_0, at_1 = top2_ids[:, 0:1] == order, top2_ids[:, 1:2] == order
    return jnp.where(at_0, x_0 / total, 0.0) + jnp.where(at_1, x_1 / total, 0.0)


def slots_and_bounds(chosen, capacity):
    count = jnp.cumsum(chosen.astype(jnp.int32), axis=1)
    slots = jnp.where(chosen & (count <= capacity), count - 1, -1)
    ends = jnp.minimum(count[:, CHUNK - 1::CHUNK], capacity)
    bounds = jnp.concatenate([jnp.zeros((ends.shape[0], 1), jnp.int32), ends], axis=1)
    return slots, bounds


def ffn_kernel(expert, row, capacity, shards, table, slots, gain, hid, gate_arg, up_arg, gate_own, g1, g2, g3,
               up_own, u1, u2, u3, down, out, weights, rows, hid_buf, act, hid_sem, w_sem):
    d_model = hid.shape[1]
    chunks = hid.shape[0] // CHUNK
    half, width = g1.shape
    units = 2 * half
    shard = table[row, chunks + 1]
    plane = table[row, chunks + 2]
    mine = pl.multiple_of(plane * half, 16)
    theirs = pl.multiple_of((1 - plane) * half, 16)

    def load_chunk(c):
        return pltpu.make_async_copy(hid.at[pl.ds(c * CHUNK, CHUNK), :], hid_buf.at[c % BUFFERS], hid_sem.at[c % BUFFERS])

    copies = []
    for w, (arg, own, others) in enumerate(((gate_arg, gate_own, (g1, g2, g3)), (up_arg, up_own, (u1, u2, u3)))):
        group = [pltpu.make_async_copy(own, weights.at[w, pl.ds(mine, half), :], w_sem.at[w])]
        col = pl.multiple_of(shard * width, 128)
        group.append(pltpu.make_async_copy(
            arg.at[expert, pl.ds(theirs, half), :], weights.at[w, pl.ds(theirs, half), pl.ds(col, width)], w_sem.at[w]))
        for k, other in enumerate(others):
            col = pl.multiple_of(((shard + k + 1) % shards) * width, 128)
            group.append(pltpu.make_async_copy(
                other, weights.at[w, pl.ds(theirs, half), pl.ds(col, width)], w_sem.at[w]))
        copies.append(group)
    copies.append([pltpu.make_async_copy(down, weights.at[2], w_sem.at[2])])

    for c in range(BUFFERS):
        load_chunk(c).start()
    for group in copies:
        for copy in group:
            copy.start()

    rows[...] = jnp.zeros_like(rows)
    for c in range(chunks):
        load_chunk(c).wait()
        low, high = table[row, c], table[row, c + 1]
        base = low // 16 * 16

        def pick(w, carry, c=c, base=base):
            start = pl.multiple_of(base + w * WINDOW, 16)
            slot = lax.broadcasted_iota(jnp.int32, (WINDOW, CHUNK), 0) + start
            select = (slots[row * chunks + c:row * chunks + c + 1, :] == slot).astype(jnp.float32).astype(jnp.bfloat16)

            def column(n, carry):
                at = pl.ds(pl.multiple_of(n * 1024, 1024), 1024)
                got = jnp.dot(select, hid_buf[c % BUFFERS, :, at], preferred_element_type=jnp.float32)
                held = rows[pl.ds(start, WINDOW), at].astype(jnp.float32)
                rows[pl.ds(start, WINDOW), at] = (held + got).astype(jnp.bfloat16)
                return carry

            return lax.fori_loop(0, d_model // 1024, column, carry)

        lax.fori_loop(0, (high - base + WINDOW - 1) // WINDOW, pick, 0)
        if c + BUFFERS < chunks:
            load_chunk(c + BUFFERS).start()

    def norm(b, carry):
        at = pl.ds(pl.multiple_of(b * 32, 32), 32)
        x = rows[at, :].astype(jnp.float32)
        mean_sq = jnp.mean(x * x, axis=-1, keepdims=True)
        rows[at, :] = (x * lax.rsqrt(mean_sq + EPS) * gain[...].astype(jnp.float32)).astype(jnp.bfloat16)
        return carry

    lax.fori_loop(0, capacity // 32, norm, 0)
    for group in copies[:2]:
        for copy in group:
            copy.wait()

    def hidden_units(at):
        x = rows[0:capacity, :]
        a = lax.dot_general(x, weights[0, at, :], NT, preferred_element_type=jnp.float32)
        b = lax.dot_general(x, weights[1, at, :], NT, preferred_element_type=jnp.float32)
        act[:, at] = (a * (1.0 / (1.0 + jnp.exp(-a))) * b).astype(jnp.bfloat16)

    tiles = units // 256

    def tile(t, carry):
        hidden_units(pl.ds(pl.multiple_of(t * 256, 256), 256))
        return carry

    lax.fori_loop(0, tiles, tile, 0)
    if units % 256:
        hidden_units(pl.ds(tiles * 256, units % 256))
    for copy in copies[2]:
        copy.wait()

    def project(n, carry):
        at = pl.ds(pl.multiple_of(n * 512, 512), 512)
        out[:, at] = jnp.dot(act[...], weights[2, :, at], preferred_element_type=jnp.float32).astype(jnp.bfloat16)
        return carry

    lax.fori_loop(0, d_model // 512, project, 0)


def expert_ffn(expert, row, capacity, table, slots, gain, hid, gate_arg, up_arg, gate, up, down):
    tokens, d_model = hid.shape
    units = 2 * gate[0].shape[0]
    shards = d_model // gate[1].shape[1]
    any_spec = pl.BlockSpec(memory_space=pl.ANY)
    vmem_spec = pl.BlockSpec(memory_space=pltpu.VMEM)
    return pl.pallas_call(
        functools.partial(ffn_kernel, expert, row, capacity, shards),
        out_shape=jax.ShapeDtypeStruct((capacity, d_model), jnp.bfloat16),
        in_specs=[pl.BlockSpec(memory_space=pltpu.SMEM), vmem_spec, vmem_spec] + [any_spec] * 12,
        out_specs=vmem_spec,
        scratch_shapes=[
            pltpu.VMEM((3, units, d_model), jnp.bfloat16),
            pltpu.VMEM((capacity + WINDOW, d_model), jnp.bfloat16),
            pltpu.VMEM((BUFFERS, CHUNK, d_model), jnp.bfloat16),
            pltpu.VMEM((capacity, units), jnp.bfloat16),
            pltpu.SemaphoreType.DMA((BUFFERS,)),
            pltpu.SemaphoreType.DMA((3,)),
        ],
        compiler_params=pltpu.CompilerParams(vmem_limit_bytes=VMEM_LIMIT),
        cost_estimate=pl.CostEstimate(flops=6 * capacity * d_model * units, transcendentals=capacity * units,
                                      bytes_accessed=2 * (3 * units + tokens + capacity) * d_model),
    )(table, slots, gain.reshape(1, d_model), hid, gate_arg, up_arg, *gate, *up, down)


def combine_kernel(capacity, first_row, count, bounds, base_ref, slots, gates, *refs):
    sources, out, acc, buf, sem = refs[:count], refs[count], refs[count + 1], refs[count + 2], refs[count + 3]
    b = pl.program_id(0)
    steps = pl.num_programs(0)
    d_model = acc.shape[1]

    def begin(step, k, w):
        low = bounds[first_row + k, step]
        return jnp.minimum(low // 16 * 16 + w * SPAN, capacity - SPAN)

    def load(step, k, w, slot):
        start = pl.multiple_of(begin(step, k, w), 16)
        return pltpu.make_async_copy(sources[k].at[pl.ds(start, SPAN), :], buf.at[slot, k], sem.at[slot, k])

    @pl.when(b == 0)
    def _():
        for k in range(count):
            load(0, k, 0, 0).start()

    @pl.when(b + 1 < steps)
    def _():
        for k in range(count):
            load(b + 1, k, 0, (b + 1) % 2).start()

    acc[...] = base_ref[...].astype(jnp.float32)
    here = b % 2
    for k in range(count):
        load(b, k, 0, here).wait()
        first = bounds[first_row + k, b] // 16 * 16

        def add(w, carry, k=k, first=first):
            @pl.when(w > 0)
            def _():
                again = load(b, k, w, here)
                again.start()
                again.wait()

            mine = slots[:, first_row + k:first_row + k + 1]
            mine = jnp.where(mine >= first + w * SPAN, mine - begin(b, k, w), -1)
            select = (mine == lax.broadcasted_iota(jnp.int32, (CHUNK, SPAN), 1)).astype(jnp.float32).astype(jnp.bfloat16)
            gate = gates[:, first_row + k:first_row + k + 1]

            def column(n, carry):
                at = pl.ds(pl.multiple_of(n * 512, 512), 512)
                acc[:, at] += gate * jnp.dot(select, buf[here, k, :, at], preferred_element_type=jnp.float32)
                return carry

            return lax.fori_loop(0, d_model // 512, column, carry)

        windows = (bounds[first_row + k, b + 1] - first + SPAN - 1) // SPAN
        lax.fori_loop(0, windows, add, 0)
    out[...] = acc[...].astype(out.dtype)


def combine(capacity, first_row, base, slots, gates, bounds, sources, out_dtype):
    tokens, d_model = base.shape
    count = len(sources)
    rows = pl.BlockSpec((CHUNK, d_model), lambda b, *_: (b, 0))
    small = pl.BlockSpec((CHUNK, slots.shape[1]), lambda b, *_: (b, 0))
    return pl.pallas_call(
        functools.partial(combine_kernel, capacity, first_row, count),
        out_shape=jax.ShapeDtypeStruct((tokens, d_model), out_dtype),
        grid_spec=pltpu.PrefetchScalarGridSpec(
            num_scalar_prefetch=1,
            grid=(tokens // CHUNK,),
            in_specs=[rows, small, small] + [pl.BlockSpec(memory_space=pl.ANY)] * count,
            out_specs=rows,
            scratch_shapes=[
                pltpu.VMEM((CHUNK, d_model), jnp.float32),
                pltpu.VMEM((2, count, SPAN, d_model), jnp.bfloat16),
                pltpu.SemaphoreType.DMA((2, count)),
            ]),
        compiler_params=pltpu.CompilerParams(vmem_limit_bytes=VMEM_LIMIT, dimension_semantics=("arbitrary",)),
        cost_estimate=pl.CostEstimate(flops=4 * tokens * SPAN * d_model * count, transcendentals=0,
                                      bytes_accessed=tokens * d_model * (4 + 2 * count)),
    )(bounds, base, slots, gates, *sources)


def local_block(hidden, norm_gain, w_router, w_gate, w_up, w_down, top2_ids):
    tok_local, d_model = hidden.shape
    num_experts = w_router.shape[1]
    capacity = (5 * tok_local + 2 * num_experts - 1) // (2 * num_experts)
    local_experts = w_gate.shape[0]
    ep_size = num_experts // local_experts
    me = lax.axis_index('ep')
    plane = lax.axis_index('dp')
    shard = lax.axis_index('fsdp')
    width = w_gate.shape[1]
    shards = d_model // width
    half = w_gate.shape[2] // 2

    def swap(value, mask):
        return lax.ppermute(value, 'ep', [(i, i ^ mask) for i in range(ep_size)])

    def swap_plane(value):
        return lax.ppermute(value, 'dp', [(0, 1), (1, 0)])

    def after(value, *earlier):
        return lax.optimization_barrier((value,) + earlier)[0]

    ids = top2_ids.T
    ids_of = [ids] + [swap(ids, m) for m in range(1, ep_size)]
    tokens = after(hidden, *ids_of)
    near = swap(tokens, 1)
    far = swap(tokens, 2)

    gate_t = w_gate.transpose(0, 2, 1)
    up_t = w_up.transpose(0, 2, 1)

    def gather_own(w_t, i):
        part = lax.dynamic_slice(w_t, (i, plane * half, 0), (1, half, width))[0]
        return lax.all_gather(part, 'fsdp', axis=1, tiled=True)

    def gather_both(w, i):
        part = lax.dynamic_slice(w, (i, 0, plane * (width // 2)), (1, w.shape[1], width // 2))[0]
        return lax.all_gather(part, ('fsdp', 'dp'), axis=1, tiled=True)

    def exchange(own):
        at = [(shard + k) % shards * width for k in range(1, shards)]
        return [own] + [swap_plane(lax.dynamic_slice_in_dim(own, start, width, axis=1)) for start in at]

    own = []
    for i in range(local_experts):
        own.append((gather_own(gate_t, i), gather_own(up_t, i), gather_both(w_down, i)))

    all_ids = jnp.concatenate(ids_of, axis=0).reshape(ep_size, 1, 2, tok_local)
    here = (local_experts * me + jnp.arange(local_experts, dtype=jnp.int32))[None, :, None]
    chosen = (all_ids[:, :, 0] == here) | (all_ids[:, :, 1] == here)
    slots, bounds = slots_and_bounds(chosen.reshape(num_experts, tok_local), capacity)
    slots = slots.reshape(num_experts * (tok_local // CHUNK), CHUNK)
    place = jnp.broadcast_to(jnp.stack([shard, plane]).astype(jnp.int32)[None, :], (num_experts, 2))
    tables = jnp.concatenate([bounds, place], axis=1)
    back = jnp.arange(num_experts, dtype=jnp.int32)
    back = local_experts * (me ^ (back % ep_size)) + back // ep_size
    chosen = (ids[0:1] == back[:, None]) | (ids[1:2] == back[:, None])
    back_slots, back_bounds = slots_and_bounds(chosen, capacity)
    back_slots = back_slots.T
    back_gates = expert_gates(norm_rows(hidden, norm_gain), w_router, top2_ids, back[None, :])
    tokens_of = [hidden, near, far, None]

    def run(i, m, weights, *earlier):
        row = m * local_experts + i
        hid = tokens_of[m] if not earlier else after(tokens_of[m], *earlier)
        out = expert_ffn(i, row, capacity, tables, slots, norm_gain, hid, gate_t, up_t, *weights)
        if not m:
            return out, out
        return out, swap(out, m)

    def put(base, i, m, backs, dtype):
        return combine(capacity, i * ep_size + m, base, back_slots, back_gates, back_bounds, backs, dtype)

    gate_a, up_a, down_a = own[0]
    weights = exchange(gate_a), exchange(up_a), down_a
    tokens_of[3] = swap(after(far, near, slots, tables, *weights[0][1:], *weights[1][1:]), 1)
    out_2, back_2 = run(0, 2, weights)
    out_3, back_3 = run(0, 3, weights, out_2)
    out_1, back_1 = run(0, 1, weights, out_3)
    out_0, back_0 = run(0, 0, weights, out_1)

    gate_b, up_b, down_b = own[1]
    weights = exchange(after(gate_b, out_0)), exchange(after(up_b, out_0))
    total = put(hidden, 0, 0, [back_0, back_1, back_2, back_3], jnp.float32)
    weights = weights + (after(down_b, total),)
    out_2, back_2 = run(1, 2, weights)
    out_3, back_3 = run(1, 3, weights, out_2)
    out_1, back_1 = run(1, 1, weights, out_3)
    out_0, back_0 = run(1, 0, weights, out_1)
    total = put(total, 1, 0, [back_0, back_1], jnp.float32)
    return put(total, 1, 2, [back_2, back_3], jnp.bfloat16)


def solution(mesh):
    tok_spec = P(('dp', 'fsdp', 'ep'), None)
    in_specs = (tok_spec, P(None), P(None, None), P('ep', 'fsdp', None), P('ep', 'fsdp', None), P('ep', None, 'fsdp'), tok_spec)
    return jax.shard_map(local_block, mesh=mesh, in_specs=in_specs, out_specs=tok_spec, check_vma=False)
```

time: 2180 us -> 1370 us (0.63)
  Pallas kernels: 0 us -> 566 us
  waiting for transfers between devices: 1230 us -> 707 us
  local copies, waits for them, and re-layouts: 473 us -> 34 us
  matrix products: 228 us -> 8.42 us
  other arithmetic: 198 us -> 18.8 us
    all_to_all x2 -> x0, waiting for transfers between devices: 863 us -> none  [the longest x1 452 us: local_block(): recv_rows = lax.all_to_all(send_rows, 'ep', 0, 1, tiled=True)]
    pallas_call x0 -> x11, Pallas kernels: none -> 566 us  [the longest x8 413 us: expert_ffn(): pl.pallas_call(functools.partial(ffn_kernel, expert, row, capacity, shard...]
    ppermute x0 -> x24, waiting for transfers between devices: none -> 443 us  [the longest x12 286 us: swap_plane(): return lax.ppermute(value, 'dp', [(0, 1), (1, 0)])]
    gather x8 -> x0, local copies, waits for them, and re-layouts: 307 us -> none  [the longest x2 203 us: take_slots(): return jnp.take(expert_rows, slot_ids, axis=0, mode='fill', fill_value=0)]
    dot_general x4 -> x1, matrix products: 228 us -> 8.42 us  [expert_gates(): logits = jnp.dot(normed, w_router, preferred_element_type=jnp.float32)]
    reduce_sum x4 -> x1, other arithmetic: 134 us -> 7.7 us  [norm_rows(): mean_sq = jnp.mean(hidden_f32 * hidden_f32, axis=-1, keepdims=True)]
    all_gather x3 -> x6, waiting for transfers between devices: 367 us -> 263 us  [the longest x4 193 us: gather_own(): return lax.all_gather(part, 'fsdp', axis=1, tiled=True)]
    convert_element_type x1 -> x0, local copies, waits for them, and re-layouts: 74.7 us -> none  [expert_block(): jnp.einsum('ecf,efd->ecd', hidden_act, down_full, preferred_element_type=...]
  transfers between devices with their start and end apart: 5 -> 30, of which waited for: 4 -> 16; matrix products, arithmetic and copies ran while one was open for 17% -> 4% of each run, Pallas kernels for 0% -> 27%
where the time goes in v1:
time: 1370 us; the launch traced here: 1360 us
  waiting for transfers between devices  707 us (52%)
  Pallas kernels  566 us (41%)
  local copies, waits for them, and re-layouts  34 us (2%)
  other arithmetic  18.8 us (1%)
  starting transfers between devices  16.1 us (1%)
  between operations  14.1 us (1%)
    pallas_call x8, Pallas kernels, expert_ffn(): pl.pallas_call(functools.partial(ffn_kernel, expert, row, capacity, shard...  413 us
    ppermute x12, waiting for transfers between devices, swap_plane(): return lax.ppermute(value, 'dp', [(0, 1), (1, 0)])  286 us
    all_gather x4, waiting for transfers between devices, gather_own(): return lax.all_gather(part, 'fsdp', axis=1, tiled=True)  193 us
    ppermute x12, waiting for transfers between devices, swap(): return lax.ppermute(value, 'ep', [(i, i ^ mask) for i in range(ep_size)])  157 us
    pallas_call x3, Pallas kernels, combine(): pl.pallas_call(functools.partial(combine_kernel, capacity, first_row, cou...  154 us
    all_gather x2, waiting for transfers between devices, gather_both(): return lax.all_gather(part, ('fsdp', 'dp'), axis=1, tiled=True)  70.3 us
  transfers between devices with their start and end apart: 30, of which 16 were waited for; matrix products, arithmetic and copies ran while one was open for 4% of the time, Pallas kernels for 27%

profile of v1, /device:TPU:2, one launch (start us, length us, event | category | flops | bytes accessed | tf_op | source)
XLA Modules:
  0.0 1364.8 jit_solution(5006791931855401753)
XLA Ops:
  6.5 3.7 dynamic-slice_bitcast_fusion.6
  10.3 3.6 dynamic-slice_bitcast_fusion.7
  14.0 3.5 constant_dynamic-slice_fusion
  17.7 1.6 collective-permute-start.1
  19.5 2.0 collective-permute-done.1
  21.5 0.9 collective-permute-done.2
  22.4 0.7 collective-permute-start.4
  23.2 92.9 %all-gather.15.cloned.1.call-done = bf16[1,688,4096]{2,1,0:T(8,128)(2,1)} async-done(((bf16[1,688,1024]{2,1,0:T(8,128)(2,1)}), bf16[1,688,4096]{2,1,0:T(8,128)(2,1)}) %all-gather.15.cloned.1.call-update) | async-done | bytes 5636112 | tf_op jit(solution)/shard_map/all_gather | solution.py:278
  116.2 3.7 dynamic-slice_bitcast_fusion
  119.9 0.6 collective-permute-start.10
  120.5 100.1 %all-gather.13.cloned.1.call-done = bf16[1,688,4096]{2,1,0:T(8,128)(2,1)} async-done(((bf16[1,688,1024]{2,1,0:T(8,128)(2,1)}), bf16[1,688,4096]{2,1,0:T(8,128)(2,1)}) %all-gather.13.cloned.1.call-update) | async-done | bytes 5636112 | tf_op jit(solution)/shard_map/all_gather | solution.py:278
  220.6 4.3 dynamic-slice_bitcast_fusion.3
  224.9 0.6 collective-permute-start.5
  225.4 1.5 collective-permute-start.6
  227.8 0.6 collective-permute-start.7
  228.5 45.6 %collective-permute-done.5.g1 = bf16[688,1024]{1,0:T(8,128)(2,1)} collective-permute-done((bf16[688,1024]{1,0:T(8,128)(2,1)}, bf16[688,1024]{1,0:T(8,128)(2,1)}, u32[]{:S(2)}, u32[]{:S(2)}) %collective-permute-start.5) | collective-permute-done | bytes 1409056 | tf_op jit(solution)/shard_map/ppermute | solution.py:262
  274.1 0.6 collective-permute-start.8
  274.6 32.7 %collective-permute-done.6.g2 = bf16[688,1024]{1,0:T(8,128)(2,1)} collective-permute-done((bf16[688,1024]{1,0:T(8,128)(2,1)}, bf16[688,1024]{1,0:T(8,128)(2,1)}, u32[]{:S(2)}, u32[]{:S(2)}) %collective-permute-start.6) | collective-permute-done | bytes 1409056 | tf_op jit(solution)/shard_map/ppermute | solution.py:262
  307.4 2.3 reduce-window.16
  310.2 1.4 copy.26
  311.7 1.2 slice.49
  313.0 0.7 and_select_fusion.slots
  313.7 54.0 %collective-permute-done.7.g3 = bf16[688,1024]{1,0:T(8,128)(2,1)} collective-permute-done((bf16[688,1024]{1,0:T(8,128)(2,1)}, bf16[688,1024]{1,0:T(8,128)(2,1)}, u32[]{:S(2)}, u32[]{:S(2)}) %collective-permute-start.7) | collective-permute-done | bytes 1409056 | tf_op jit(solution)/shard_map/ppermute | solution.py:262
  367.7 57.3 %collective-permute-done.8.u1 = bf16[688,1024]{1,0:T(8,128)(2,1)} collective-permute-done((bf16[688,1024]{1,0:T(8,128)(2,1)S(1)}, bf16[688,1024]{1,0:T(8,128)(2,1)}, u32[]{:S(2)}, u32[]{:S(2)}) %collective-permute-start.8) | collective-permute-done | bytes 1409056 | tf_op jit(solution)/shard_map/ppermute | solution.py:262
  425.0 29.1 %collective-permute-done.9.u2 = bf16[688,1024]{1,0:T(8,128)(2,1)} collective-permute-done((bf16[688,1024]{1,0:T(8,128)(2,1)S(1)}, bf16[688,1024]{1,0:T(8,128)(2,1)}, u32[]{:S(2)}, u32[]{:S(2)}) %collective-permute-start.9) | collective-permute-done | bytes 1409056 | tf_op jit(solution)/shard_map/ppermute | solution.py:262
  454.3 0.5 all-gather.23.cloned.1.call-update
  454.8 0.6 reshape.167.gain
  455.5 2.3 reduce-window.14
  458.8 0.8 concatenate.9.clone.bounds
  459.7 7.7 fusion
  467.4 0.7 copy.30.table
  468.1 52.0 %shard_map.73 = bf16[640,4096]{1,0:T(8,128)(2,1)} custom-call(s32[8,11]{1,0:T(8,128)} %copy.30.table, s32[64,256]{1,0:T(8,128)} %and_select_fusion.slots, bf16[1,4096]{1,0:T(2,128)(2,1)} %reshape.167.gain, bf16[2048,4096]{1,0:T(8,128)(2,1)} %collective-permute-done.4.hid, bf16[2,1376,1024]{2,1,0:T(8,128)(2,1)} %bitcast.69, bf16[2,1376,1024]{2,1,0:T(8,128)(2,1)} %bitcast.77, ...), custom_call_target="tpu_custom_call" | custom-call | flops 21642608640 | bytes 55836672 | tf_op jit(solution)/shard_map/pallas_call | solution.py:148
  520.0 0.6 collective-permute-start.13
  520.6 51.6 %shard_map.74 = bf16[640,4096]{1,0:T(8,128)(2,1)} custom-call(s32[8,11]{1,0:T(8,128)} %copy.30.table, s32[64,256]{1,0:T(8,128)} %and_select_fusion.slots, bf16[1,4096]{1,0:T(2,128)(2,1)} %reshape.167.gain, bf16[2048,4096]{1,0:T(8,128)(2,1)} %collective-permute-done.11.hid, bf16[2,1376,1024]{2,1,0:T(8,128)(2,1)} %bitcast.70, bf16[2,1376,1024]{2,1,0:T(8,128)(2,1)} %bitcast.78, ...), custom_call_target="tpu_custom_call" | custom-call | flops 21642608640 | bytes 55836672 | tf_op jit(solution)/shard_map/pallas_call | solution.py:148
  572.3 0.5 collective-permute-start.14
  572.8 51.6 %shard_map.75 = bf16[640,4096]{1,0:T(8,128)(2,1)} custom-call(s32[8,11]{1,0:T(8,128)} %copy.30.table, s32[64,256]{1,0:T(8,128)} %and_select_fusion.slots, bf16[1,4096]{1,0:T(2,128)(2,1)} %reshape.167.gain, bf16[2048,4096]{1,0:T(8,128)(2,1)} %collective-permute-done.3.hid, bf16[2,1376,1024]{2,1,0:T(8,128)(2,1)} %bitcast.71, bf16[2,1376,1024]{2,1,0:T(8,128)(2,1)} %bitcast.79, ...), custom_call_target="tpu_custom_call" | custom-call | flops 21642608640 | bytes 55836672 | tf_op jit(solution)/shard_map/pallas_call | solution.py:148
  624.7 8.4 select_reduce_fusion.1
  633.1 51.7 %shard_map.76.refs_0_ = bf16[640,4096]{1,0:T(8,128)(2,1)} custom-call(s32[8,11]{1,0:T(8,128)} %copy.30.table, s32[64,256]{1,0:T(8,128)} %and_select_fusion.slots, bf16[1,4096]{1,0:T(2,128)(2,1)} %reshape.167.gain, bf16[2048,4096]{1,0:T(8,128)(2,1)} %hid.1, bf16[2,1376,1024]{2,1,0:T(8,128)(2,1)} %bitcast.72, bf16[2,1376,1024]{2,1,0:T(8,128)(2,1)} %bitcast.80, ...), custom_call_target="tpu_custom_call" | custom-call | flops 21642608640 | bytes 55836672 | tf_op jit(solution)/shard_map/pallas_call | solution.py:148
  684.9 4.3 constant_dynamic-slice_fusion.4
  689.1 1.3 collective-permute-start.15
  690.5 2.6 select_add_fusion.gates
  693.1 2.3 select_bitcast_fusion.slots
  695.4 0.7 collective-permute-start.16
  696.1 4.3 constant_dynamic-slice_fusion.1
  700.4 1.3 collective-permute-start.17
  701.7 21.2 %collective-permute-done.15.g1 = bf16[688,1024]{1,0:T(8,128)(2,1)} collective-permute-done((bf16[688,1024]{1,0:T(8,128)(2,1)S(1)}, bf16[688,1024]{1,0:T(8,128)(2,1)}, u32[]{:S(2)}, u32[]{:S(2)}) %collective-permute-start.15) | collective-permute-done | bytes 1409056 | tf_op jit(solution)/shard_map/ppermute | solution.py:262
  723.0 1.3 collective-permute-start.18
  724.3 0.7 collective-permute-start.19
  725.0 22.8 %collective-permute-done.14.refs_3_ = bf16[640,4096]{1,0:T(8,128)(2,1)} collective-permute-done((bf16[640,4096]{1,0:T(8,128)(2,1)}, bf16[640,4096]{1,0:T(8,128)(2,1)}, u32[]{:S(2)}, u32[]{:S(2)}) %collective-permute-start.14) | collective-permute-done | bytes 5242912 | tf_op jit(solution)/shard_map/ppermute | solution.py:259
  747.8 0.6 collective-permute-start.20
  748.4 69.4 %shard_map.77.base_ref = f32[2048,4096]{1,0:T(8,128)} custom-call(s32[8,9]{1,0:T(8,128)} %concatenate.9.clone.bounds, bf16[2048,4096]{1,0:T(8,128)(2,1)} %hid.1, s32[2048,8]{1,0:T(8,128)} %select_bitcast_fusion.slots, f32[2048,8]{1,0:T(8,128)} %select_add_fusion.gates, bf16[640,4096]{1,0:T(8,128)(2,1)} %shard_map.76.refs_0_, ...), custom_call_target="tpu_custom_call" | custom-call | flops 21474836480 | bytes 100663296 | tf_op jit(solution)/shard_map/pallas_call | solution.py:226
  817.9 70.3 %all-gather.23.cloned.1.call-done = bf16[1,1376,4096]{2,1,0:T(8,128)(2,1)} async-done(((bf16[1,1376,512]{2,1,0:T(8,128)(2,1)}), bf16[1,1376,4096]{2,1,0:T(8,128)(2,1)}) %all-gather.23.cloned.1.call-update) | async-done | bytes 11272208 | tf_op jit(solution)/shard_map/all_gather | solution.py:282
  888.2 16.0 %collective-permute-done.19.u2 = bf16[688,1024]{1,0:T(8,128)(2,1)} collective-permute-done((bf16[688,1024]{1,0:T(8,128)(2,1)}, bf16[688,1024]{1,0:T(8,128)(2,1)}, u32[]{:S(2)}, u32[]{:S(2)}) %collective-permute-start.19) | collective-permute-done | bytes 1409056 | tf_op jit(solution)/shard_map/ppermute | solution.py:262
  904.2 29.5 %collective-permute-done.20.u3 = bf16[688,1024]{1,0:T(8,128)(2,1)} collective-permute-done((bf16[688,1024]{1,0:T(8,128)(2,1)}, bf16[688,1024]{1,0:T(8,128)(2,1)}, u32[]{:S(2)}, u32[]{:S(2)}) %collective-permute-start.20) | collective-permute-done | bytes 1409056 | tf_op jit(solution)/shard_map/ppermute | solution.py:262
  933.6 51.7 %shard_map.78 = bf16[640,4096]{1,0:T(8,128)(2,1)} custom-call(s32[8,11]{1,0:T(8,128)} %copy.30.table, s32[64,256]{1,0:T(8,128)} %and_select_fusion.slots, bf16[1,4096]{1,0:T(2,128)(2,1)} %reshape.167.gain, bf16[2048,4096]{1,0:T(8,128)(2,1)} %collective-permute-done.4.hid, bf16[2,1376,1024]{2,1,0:T(8,128)(2,1)} %bitcast.73, bf16[2,1376,1024]{2,1,0:T(8,128)(2,1)} %bitcast.81, ...), custom_call_target="tpu_custom_call" | custom-call | flops 21642608640 | bytes 55836672 | tf_op jit(solution)/shard_map/pallas_call | solution.py:148
  985.4 51.3 %shard_map.79 = bf16[640,4096]{1,0:T(8,128)(2,1)} custom-call(s32[8,11]{1,0:T(8,128)} %copy.30.table, s32[64,256]{1,0:T(8,128)} %and_select_fusion.slots, bf16[1,4096]{1,0:T(2,128)(2,1)} %reshape.167.gain, bf16[2048,4096]{1,0:T(8,128)(2,1)} %collective-permute-done.11.hid, bf16[2,1376,1024]{2,1,0:T(8,128)(2,1)} %bitcast.74, bf16[2,1376,1024]{2,1,0:T(8,128)(2,1)} %bitcast.82, ...), custom_call_target="tpu_custom_call" | custom-call | flops 21642608640 | bytes 55836672 | tf_op jit(solution)/shard_map/pallas_call | solution.py:148
  1036.7 51.4 %shard_map.80 = bf16[640,4096]{1,0:T(8,128)(2,1)} custom-call(s32[8,11]{1,0:T(8,128)} %copy.30.table, s32[64,256]{1,0:T(8,128)} %and_select_fusion.slots, bf16[1,4096]{1,0:T(2,128)(2,1)} %reshape.167.gain, bf16[2048,4096]{1,0:T(8,128)(2,1)} %collective-permute-done.3.hid, bf16[2,1376,1024]{2,1,0:T(8,128)(2,1)} %bitcast.75, bf16[2,1376,1024]{2,1,0:T(8,128)(2,1)} %bitcast.83, ...), custom_call_target="tpu_custom_call" | custom-call | flops 21642608640 | bytes 55836672 | tf_op jit(solution)/shard_map/pallas_call | solution.py:148
  1088.2 1.0 collective-permute-start.23
  1089.2 1.1 collective-permute-start.22
  1090.3 51.6 %shard_map.81.refs_0_ = bf16[640,4096]{1,0:T(8,128)(2,1)} custom-call(s32[8,11]{1,0:T(8,128)} %copy.30.table, s32[64,256]{1,0:T(8,128)} %and_select_fusion.slots, bf16[1,4096]{1,0:T(2,128)(2,1)} %reshape.167.gain, bf16[2048,4096]{1,0:T(8,128)(2,1)} %hid.1, bf16[2,1376,1024]{2,1,0:T(8,128)(2,1)} %bitcast.76, bf16[2,1376,1024]{2,1,0:T(8,128)(2,1)} %bitcast.84, ...), custom_call_target="tpu_custom_call" | custom-call | flops 21642608640 | bytes 55836672 | tf_op jit(solution)/shard_map/pallas_call | solution.py:148
  1141.9 42.6 %shard_map.82.base_ref = f32[2048,4096]{1,0:T(8,128)} custom-call(s32[8,9]{1,0:T(8,128)} %concatenate.9.clone.bounds, f32[2048,4096]{1,0:T(8,128)} %shard_map.77.base_ref, s32[2048,8]{1,0:T(8,128)} %select_bitcast_fusion.slots, f32[2048,8]{1,0:T(8,128)} %select_add_fusion.gates, bf16[640,4096]{1,0:T(8,128)(2,1)} %shard_map.81.refs_0_, ...), custom_call_target="tpu_custom_call" | custom-call | flops 10737418240 | bytes 67108864 | tf_op jit(solution)/shard_map/pallas_call | solution.py:226
  1184.5 18.7 %collective-permute-done.23.refs_1_ = bf16[640,4096]{1,0:T(8,128)(2,1)} collective-permute-done((bf16[640,4096]{1,0:T(8,128)(2,1)}, bf16[640,4096]{1,0:T(8,128)(2,1)}, u32[]{:S(2)}, u32[]{:S(2)}) %collective-permute-start.23) | collective-permute-done | bytes 5242912 | tf_op jit(solution)/shard_map/ppermute | solution.py:259
  1203.3 113.0 %collective-permute-done.22.refs_0_ = bf16[640,4096]{1,0:T(8,128)(2,1)} collective-permute-done((bf16[640,4096]{1,0:T(8,128)(2,1)}, bf16[640,4096]{1,0:T(8,128)(2,1)}, u32[]{:S(2)}, u32[]{:S(2)}) %collective-permute-start.22) | collective-permute-done | bytes 5242912 | tf_op jit(solution)/shard_map/ppermute | solution.py:259
  1316.2 41.5 %shard_map.83 = bf16[2048,4096]{1,0:T(8,128)(2,1)} custom-call(s32[8,9]{1,0:T(8,128)} %concatenate.9.clone.bounds, f32[2048,4096]{1,0:T(8,128)} %shard_map.82.base_ref, s32[2048,8]{1,0:T(8,128)} %select_bitcast_fusion.slots, f32[2048,8]{1,0:T(8,128)} %select_add_fusion.gates, bf16[640,4096]{1,0:T(8,128)(2,1)} %collective-permute-done.22.refs_0_, ...), custom_call_target="tpu_custom_call" | custom-call | flops 10737418240 | bytes 67108864 | tf_op jit(solution)/shard_map/pallas_call | solution.py:226
  (85 shorter events, 3.8 us)
Async XLA Ops:
  6.5 618.2 %copy-start = (bf16[4096,8]{0,1:T(8,128)(2,1)S(1)}, bf16[4096,8]{0,1:T(8,128)(2,1)}, u32[]{:S(2)}) copy-start(bf16[4096,8]{0,1:T(8,128)(2,1)} %param.9) | copy-start | bytes 196612
  6.5 109.6 %all-gather.15.cloned.1.call-start = ((), (), s32[]{:S(2)}) async-start(), calls=%async_computation.1 | async-start | bytes 7045120 | tf_op jit(solution)/shard_map/all_gather | solution.py:278
  10.3 210.3 %all-gather.13.cloned.1.call-start = ((), (), s32[]{:S(2)}) async-start(), calls=%async_computation | async-start | bytes 7045120 | tf_op jit(solution)/shard_map/all_gather | solution.py:278
  13.9 3.7 copy-start.4
  13.9 454.1 %all-gather.17.cloned.1.call-start = ((), (), s32[]{:S(2)}) async-start(), calls=%async_computation.2 | async-start | bytes 12681216 | tf_op jit(solution)/shard_map/all_gather | solution.py:282
  17.5 667.3 %all-gather.19.cloned.1.call-start = ((), (), s32[]{:S(2)}) async-start(), calls=%async_computation.3 | async-start | bytes 7045120 | tf_op jit(solution)/shard_map/all_gather | solution.py:278
  17.6 1.9 collective-permute-start
  17.7 3.8 collective-permute-start.1
  19.3 3.2 collective-permute-start.2
  22.4 431.8 %collective-permute-start.4 = (bf16[2048,4096]{1,0:T(8,128)(2,1)}, bf16[2048,4096]{1,0:T(8,128)(2,1)}, u32[]{:S(2)}, u32[]{:S(2)}) collective-permute-start(bf16[2048,4096]{1,0:T(8,128)(2,1)} %hid.1), channel_id=1, source_target_pairs={{0,2},{1,3},{2,0},{3,1},{4,6},{5,7},{6,4},{7,5},{8,10},{9,11},{10,... | collective-permute-start | bytes 50331656 | tf_op jit(solution)/shard_map/ppermute | solution.py:259
  23.1 431.1 %collective-permute-start.3 = (bf16[2048,4096]{1,0:T(8,128)(2,1)}, bf16[2048,4096]{1,0:T(8,128)(2,1)}, u32[]{:S(2)}, u32[]{:S(2)}) collective-permute-start(bf16[2048,4096]{1,0:T(8,128)(2,1)} %hid.1), channel_id=1, source_target_pairs={{0,1},{1,0},{2,3},{3,2},{4,5},{5,4},{6,7},{7,6},{8,9},{9,8},{10,11... | collective-permute-start | bytes 50331656 | tf_op jit(solution)/shard_map/ppermute | solution.py:259
  23.1 672.9 %all-gather.21.cloned.1.call-start = ((), (), s32[]{:S(2)}) async-start(), calls=%async_computation.4 | async-start | bytes 7045120 | tf_op jit(solution)/shard_map/all_gather | solution.py:278
  119.9 107.9 %collective-permute-start.10 = (bf16[688,1024]{1,0:T(8,128)(2,1)}, bf16[688,1024]{1,0:T(8,128)(2,1)}, u32[]{:S(2)}, u32[]{:S(2)}) collective-permute-start(bf16[688,1024]{1,0:T(8,128)(2,1)} %get-tuple-element.43), channel_id=1, source_target_pairs={{0,16},{16,0},{1,17},{17,1},{2,18},{18,2},{3,19},{19,3},{4,20},{20... | collective-permute-start | bytes 4227080 | tf_op jit(solution)/shard_map/ppermute | solution.py:262
  224.9 229.9 %copy-start.5 = (bf16[4096]{0:T(1024)(128)(2,1)S(1)}, bf16[4096]{0:T(1024)(128)(2,1)}, u32[]{:S(2)}) copy-start(bf16[4096]{0:T(1024)(128)(2,1)} %param.8) | copy-start | bytes 24580
  224.9 49.2 %collective-permute-start.5 = (bf16[688,1024]{1,0:T(8,128)(2,1)}, bf16[688,1024]{1,0:T(8,128)(2,1)}, u32[]{:S(2)}, u32[]{:S(2)}) collective-permute-start(bf16[688,1024]{1,0:T(8,128)(2,1)} %get-tuple-element.48), channel_id=1, source_target_pairs={{0,16},{16,0},{1,17},{17,1},{2,18},{18,2},{3,19},{19,3},{4,20},{20... | collective-permute-start | bytes 4227080 | tf_op jit(solution)/shard_map/ppermute | solution.py:262
  225.4 81.9 %collective-permute-start.6 = (bf16[688,1024]{1,0:T(8,128)(2,1)}, bf16[688,1024]{1,0:T(8,128)(2,1)}, u32[]{:S(2)}, u32[]{:S(2)}) collective-permute-start(bf16[688,1024]{1,0:T(8,128)(2,1)} %get-tuple-element.47), channel_id=1, source_target_pairs={{0,16},{16,0},{1,17},{17,1},{2,18},{18,2},{3,19},{19,3},{4,20},{20... | collective-permute-start | bytes 4227080 | tf_op jit(solution)/shard_map/ppermute | solution.py:262
  227.8 139.9 %collective-permute-start.7 = (bf16[688,1024]{1,0:T(8,128)(2,1)}, bf16[688,1024]{1,0:T(8,128)(2,1)}, u32[]{:S(2)}, u32[]{:S(2)}) collective-permute-start(bf16[688,1024]{1,0:T(8,128)(2,1)} %get-tuple-element.46), channel_id=1, source_target_pairs={{0,16},{16,0},{1,17},{17,1},{2,18},{18,2},{3,19},{19,3},{4,20},{20... | collective-permute-start | bytes 4227080 | tf_op jit(solution)/shard_map/ppermute | solution.py:262
  274.1 151.0 %collective-permute-start.8 = (bf16[688,1024]{1,0:T(8,128)(2,1)S(1)}, bf16[688,1024]{1,0:T(8,128)(2,1)}, u32[]{:S(2)}, u32[]{:S(2)}) collective-permute-start(bf16[688,1024]{1,0:T(8,128)(2,1)S(1)} %get-tuple-element.45), channel_id=1, source_target_pairs={{0,16},{16,0},{1,17},{17,1},{2,18},{18,2},{3,19},{19,3},{4,20},{20... | collective-permute-start | bytes 4227080 | tf_op jit(solution)/shard_map/ppermute | solution.py:262
  307.3 146.9 %collective-permute-start.9 = (bf16[688,1024]{1,0:T(8,128)(2,1)S(1)}, bf16[688,1024]{1,0:T(8,128)(2,1)}, u32[]{:S(2)}, u32[]{:S(2)}) collective-permute-start(bf16[688,1024]{1,0:T(8,128)(2,1)S(1)} %get-tuple-element.44), channel_id=1, source_target_pairs={{0,16},{16,0},{1,17},{17,1},{2,18},{18,2},{3,19},{19,3},{4,20},{20... | collective-permute-start | bytes 4227080 | tf_op jit(solution)/shard_map/ppermute | solution.py:262
  454.2 66.4 %collective-permute-start.11 = (bf16[2048,4096]{1,0:T(8,128)(2,1)}, bf16[2048,4096]{1,0:T(8,128)(2,1)}, u32[]{:S(2)}, u32[]{:S(2)}) collective-permute-start(bf16[2048,4096]{1,0:T(8,128)(2,1)} %collective-permute-done.4.hid), channel_id=1, source_target_pairs={{0,1},{1,0},{2,3},{3,2},{4,5},{5,4},{6,7},{7,6},{8,9},{9,8},{10,11... | collective-permute-start | bytes 50331656 | tf_op jit(solution)/shard_map/ppermute | solution.py:259
  454.2 433.9 %all-gather.23.cloned.1.call-start = ((), (), s32[]{:S(2)}) async-start(), calls=%async_computation.5 | async-start | bytes 12681216 | tf_op jit(solution)/shard_map/all_gather | solution.py:282
  458.7 8.7 copy-start.2
  520.0 180.4 %collective-permute-start.13 = (bf16[640,4096]{1,0:T(8,128)(2,1)}, bf16[640,4096]{1,0:T(8,128)(2,1)}, u32[]{:S(2)}, u32[]{:S(2)}) collective-permute-start(bf16[640,4096]{1,0:T(8,128)(2,1)} %shard_map.73), channel_id=1, source_target_pairs={{0,2},{1,3},{2,0},{3,1},{4,6},{5,7},{6,4},{7,5},{8,10},{9,11},{10,... | collective-permute-start | bytes 15728648 | tf_op jit(solution)/shard_map/ppermute | solution.py:259
  572.3 175.6 %collective-permute-start.14 = (bf16[640,4096]{1,0:T(8,128)(2,1)}, bf16[640,4096]{1,0:T(8,128)(2,1)}, u32[]{:S(2)}, u32[]{:S(2)}) collective-permute-start(bf16[640,4096]{1,0:T(8,128)(2,1)} %shard_map.74), channel_id=1, source_target_pairs={{0,3},{1,2},{2,1},{3,0},{4,7},{5,6},{6,5},{7,4},{8,11},{9,10},{10,... | collective-permute-start | bytes 15728648 | tf_op jit(solution)/shard_map/ppermute | solution.py:259
  624.4 100.0 %collective-permute-start.12 = (bf16[640,4096]{1,0:T(8,128)(2,1)}, bf16[640,4096]{1,0:T(8,128)(2,1)}, u32[]{:S(2)}, u32[]{:S(2)}) collective-permute-start(bf16[640,4096]{1,0:T(8,128)(2,1)} %shard_map.75), channel_id=1, source_target_pairs={{0,1},{1,0},{2,3},{3,2},{4,5},{5,4},{6,7},{7,6},{8,9},{9,8},{10,11... | collective-permute-start | bytes 15728648 | tf_op jit(solution)/shard_map/ppermute | solution.py:259
  684.8 8.3 copy-start.3
  689.1 33.9 %collective-permute-start.15 = (bf16[688,1024]{1,0:T(8,128)(2,1)S(1)}, bf16[688,1024]{1,0:T(8,128)(2,1)}, u32[]{:S(2)}, u32[]{:S(2)}) collective-permute-start(bf16[688,1024]{1,0:T(8,128)(2,1)S(1)} %get-tuple-element.40), channel_id=1, source_target_pairs={{0,16},{16,0},{1,17},{17,1},{2,18},{18,2},{3,19},{19,3},{4,20},{20... | collective-permute-start | bytes 4227080 | tf_op jit(solution)/shard_map/ppermute | solution.py:262
  695.4 192.8 %collective-permute-start.16 = (bf16[688,1024]{1,0:T(8,128)(2,1)}, bf16[688,1024]{1,0:T(8,128)(2,1)}, u32[]{:S(2)}, u32[]{:S(2)}) collective-permute-start(bf16[688,1024]{1,0:T(8,128)(2,1)} %get-tuple-element.39), channel_id=1, source_target_pairs={{0,16},{16,0},{1,17},{17,1},{2,18},{18,2},{3,19},{19,3},{4,20},{20... | collective-permute-start | bytes 4227080 | tf_op jit(solution)/shard_map/ppermute | solution.py:262
  700.4 187.8 %collective-permute-start.17 = (bf16[688,1024]{1,0:T(8,128)(2,1)}, bf16[688,1024]{1,0:T(8,128)(2,1)}, u32[]{:S(2)}, u32[]{:S(2)}) collective-permute-start(bf16[688,1024]{1,0:T(8,128)(2,1)} %get-tuple-element.38), channel_id=1, source_target_pairs={{0,16},{16,0},{1,17},{17,1},{2,18},{18,2},{3,19},{19,3},{4,20},{20... | collective-permute-start | bytes 4227080 | tf_op jit(solution)/shard_map/ppermute | solution.py:262
  723.0 165.2 %collective-permute-start.18 = (bf16[688,1024]{1,0:T(8,128)(2,1)}, bf16[688,1024]{1,0:T(8,128)(2,1)}, u32[]{:S(2)}, u32[]{:S(2)}) collective-permute-start(bf16[688,1024]{1,0:T(8,128)(2,1)} %get-tuple-element.35), channel_id=1, source_target_pairs={{0,16},{16,0},{1,17},{17,1},{2,18},{18,2},{3,19},{19,3},{4,20},{20... | collective-permute-start | bytes 4227080 | tf_op jit(solution)/shard_map/ppermute | solution.py:262
  724.3 179.8 %collective-permute-start.19 = (bf16[688,1024]{1,0:T(8,128)(2,1)}, bf16[688,1024]{1,0:T(8,128)(2,1)}, u32[]{:S(2)}, u32[]{:S(2)}) collective-permute-start(bf16[688,1024]{1,0:T(8,128)(2,1)} %get-tuple-element.34), channel_id=1, source_target_pairs={{0,16},{16,0},{1,17},{17,1},{2,18},{18,2},{3,19},{19,3},{4,20},{20... | collective-permute-start | bytes 4227080 | tf_op jit(solution)/shard_map/ppermute | solution.py:262
  747.8 185.8 %collective-permute-start.20 = (bf16[688,1024]{1,0:T(8,128)(2,1)}, bf16[688,1024]{1,0:T(8,128)(2,1)}, u32[]{:S(2)}, u32[]{:S(2)}) collective-permute-start(bf16[688,1024]{1,0:T(8,128)(2,1)} %get-tuple-element.33), channel_id=1, source_target_pairs={{0,16},{16,0},{1,17},{17,1},{2,18},{18,2},{3,19},{19,3},{4,20},{20... | collective-permute-start | bytes 4227080 | tf_op jit(solution)/shard_map/ppermute | solution.py:262
  1088.1 53.8 %collective-permute-start.21 = (bf16[640,4096]{1,0:T(8,128)(2,1)}, bf16[640,4096]{1,0:T(8,128)(2,1)}, u32[]{:S(2)}, u32[]{:S(2)}) collective-permute-start(bf16[640,4096]{1,0:T(8,128)(2,1)} %shard_map.80), channel_id=1, source_target_pairs={{0,1},{1,0},{2,3},{3,2},{4,5},{5,4},{6,7},{7,6},{8,9},{9,8},{10,11... | collective-permute-start | bytes 15728648 | tf_op jit(solution)/shard_map/ppermute | solution.py:259
  1088.2 115.1 %collective-permute-start.23 = (bf16[640,4096]{1,0:T(8,128)(2,1)}, bf16[640,4096]{1,0:T(8,128)(2,1)}, u32[]{:S(2)}, u32[]{:S(2)}) collective-permute-start(bf16[640,4096]{1,0:T(8,128)(2,1)} %shard_map.79), channel_id=1, source_target_pairs={{0,3},{1,2},{2,1},{3,0},{4,7},{5,6},{6,5},{7,4},{8,11},{9,10},{10,... | collective-permute-start | bytes 15728648 | tf_op jit(solution)/shard_map/ppermute | solution.py:259
  1089.2 227.1 %collective-permute-start.22 = (bf16[640,4096]{1,0:T(8,128)(2,1)}, bf16[640,4096]{1,0:T(8,128)(2,1)}, u32[]{:S(2)}, u32[]{:S(2)}) collective-permute-start(bf16[640,4096]{1,0:T(8,128)(2,1)} %shard_map.78), channel_id=1, source_target_pairs={{0,2},{1,3},{2,0},{3,1},{4,6},{5,7},{6,4},{7,5},{8,10},{9,11},{10,... | collective-permute-start | bytes 15728648 | tf_op jit(solution)/shard_map/ppermute | solution.py:259
  1316.2 41.5 %copy-start.1 = (bf16[4096,8]{0,1:T(8,128)(2,1)S(1)}, bf16[4096,8]{0,1:T(8,128)(2,1)}, u32[]{:S(2)}) copy-start(bf16[4096,8]{0,1:T(8,128)(2,1)} %param.9) | copy-start | bytes 196612
Sparse Core Ops, SparseCore 0:
  10.4 105.7 all-gather.14
  117.7 102.7 all-gather.12
  222.6 233.5 all-gather.16
  457.6 103.6 all-gather.18
  562.7 102.7 all-gather.20
  667.4 220.6 all-gather.22
